TPU v7x, 32 devices: a whole 2x2x4 slice. The times are simulated.
32 devices in a mesh: row: 8 (over y, x, core), grp: 4 (over z).
Axes of the slice: x: 2, y: 2, z: 4, core: 2. Of those that a mesh axis runs over, the one named last changes fastest.
Arguments:
- positions: float32 [3, 1024], replicated, may hold values from -0.05 to 9.35, as said below
- detuning: float32 [1024], replicated, may hold values from -1 to 1
- populations: float32 [1024], P('row'), may hold values from 0 to 1
- base: float32 [2, 64, 1024], P(None, 'grp', 'row'), may hold values from -6 to 6
- section: float32 [2, 64, 1024], P(None, 'grp', 'row'), may hold values from -6 to 6
- accum: float32 [2, 64, 1024], P(None, 'grp', 'row'), may hold values from -3 to 3
Outputs:
- next_input: float32 [2, 64, 1024], P(None, 'grp', 'row')
- accum_out: float32 [2, 64, 1024], P(None, 'grp', 'row')
Inputs may be any that keep to these rules, and one draw needn't show every extreme that they name: `positions`: emitter n sits near the lattice point 0.3 * (n % 32, (n // 32) % 32, n // 1024), displaced by at most 0.05 in each coordinate.
All inputs are finite; a program needn't handle non-finite values.
Results may differ from a plain program's by a relative error of at most 0.0003.
Values sent between devices are 32-bit elements; how exact they have to be, the bound alone decides.
A program may use at most 64 MiB of HBM per device.

v0:
```python
import functools
import math

import jax
import jax.numpy as jnp
from jax import lax
from jax.experimental import pallas as pl
from jax.experimental.pallas import tpu as pltpu
from jax.sharding import PartitionSpec as P

TIME_STEP = 0.2
CHUNK = 32
PAD = 16

SIN_COEFFS = (
    6.283185302511502,
    -41.3417004053172,
    81.60513138578366,
    -76.7030153536576,
    42.02592698454004,
    -14.89984666366821,
    3.2381375046186873,
)
COS_COEFFS = (
    0.9999999890590228,
    -19.739204499453827,
    64.9391174598908,
    -85.45013953079768,
    60.16763095026347,
    -25.967599245923736,
    6.52865815775625,
)


def horner(coeffs, t):
    total = coeffs[-1] * t + coeffs[-2]
    for value in coeffs[-3::-1]:
        total = total * t + value
    return total


def coupling(cols, rows, diag):
    dx = cols[0] - rows[0]
    dy = cols[1] - rows[1]
    dz = cols[2] - rows[2]
    dz_sq = dz * dz
    dist_sq = dx * dx + dy * dy + dz_sq
    if diag is not None:
        dist_sq = jnp.where(diag, 1.0, dist_sq)
    inv = lax.rsqrt(dist_sq)
    dist = dist_sq * inv
    frac = dist - jnp.round(dist)
    t = frac * frac
    sine = frac * horner(SIN_COEFFS, t)
    cosine = horner(COS_COEFFS, t)
    aligned = dz_sq * (inv * inv)
    mix = 1.0 - 3.0 * aligned
    u = inv * (0.5 / math.pi)
    quad_imag = u * mix
    quad_real = (1.0 - aligned) - u * quad_imag
    scale = -0.75 * u
    amp_real = scale * quad_real
    amp_imag = scale * quad_imag
    h_real = amp_real * cosine - amp_imag * sine
    h_imag = amp_real * sine + amp_imag * cosine
    if diag is not None:
        h_real = jnp.where(diag, 0.0, h_real)
        h_imag = jnp.where(diag, 0.0, h_imag)
    return h_real, h_imag


def split(x):
    hi = x.astype(jnp.bfloat16)
    return hi, (x - hi.astype(jnp.float32)).astype(jnp.bfloat16)


def bdot(a, b):
    return jnp.dot(a, b, preferred_element_type=jnp.float32)


def kernel(
    n_row,
    n_grp,
    pos_in,
    det_in,
    pop_in,
    sec_in,
    out_ref,
    pos_ref,
    det_ref,
    pop_ref,
    sec_ref,
    pos_t,
    rhs_hi,
    rhs_lo,
    row_buf,
    pop_buf,
    grp_buf,
    sec_send,
    sec_recv,
    pop_send,
    pop_recv,
    grp_send,
    grp_recv,
    load_sem,
):
    loads = []
    for i, (src, dst) in enumerate(((sec_in, sec_ref), (pop_in, pop_ref), (pos_in, pos_ref), (det_in, det_ref))):
        load = pltpu.make_async_copy(src, dst, load_sem.at[i])
        load.start()
        loads.append(load)
    me = lax.axis_index("row")
    mine = lax.axis_index("grp")
    cols, width = sec_ref.shape[1], sec_ref.shape[2]
    slab = cols * n_grp

    def row_peer(s):
        return lax.rem(me + s, n_row)

    def grp_peer(s):
        return lax.rem(mine + s, n_grp)

    barrier = pltpu.get_barrier_semaphore()
    for s in range(1, n_row):
        pl.semaphore_signal(barrier, inc=1, device_id={"row": row_peer(s)}, device_id_type=pl.DeviceIdType.MESH)
    for s in range(1, n_grp):
        pl.semaphore_signal(barrier, inc=1, device_id={"grp": grp_peer(s)}, device_id_type=pl.DeviceIdType.MESH)

    loads[0].wait()
    loads[1].wait()
    pl.semaphore_wait(barrier, n_row + n_grp - 2)

    row_copies = []
    for s in range(1, n_row):
        target = {"row": row_peer(s)}
        copy = pltpu.make_async_remote_copy(
            sec_ref, row_buf.at[s], sec_send.at[s], sec_recv.at[s], device_id=target, device_id_type=pl.DeviceIdType.MESH
        )
        copy.start()
        pop_copy = pltpu.make_async_remote_copy(
            pop_ref, pop_buf.at[s], pop_send.at[s], pop_recv.at[s], device_id=target, device_id_type=pl.DeviceIdType.MESH
        )
        pop_copy.start()
        row_copies.append((copy, pop_copy))
    grp_copies = []
    for s in range(1, n_grp):
        copy = pltpu.make_async_remote_copy(
            sec_ref,
            grp_buf.at[s],
            grp_send.at[s],
            grp_recv.at[s],
            device_id={"grp": grp_peer(s)},
            device_id_type=pl.DeviceIdType.MESH,
        )
        copy.start()
        grp_copies.append(copy)

    loads[2].wait()
    loads[3].wait()
    for b in range(n_row):
        part = pos_ref[:, b * width : (b + 1) * width]
        tall = jnp.concatenate([part, jnp.zeros((5, width), jnp.float32)], axis=0)
        pos_t[b * width : (b + 1) * width, :] = jnp.transpose(tall)

    my_start = pl.multiple_of(me * width, width)
    rows = [pos_ref[d : d + 1, pl.ds(my_start, width)] for d in range(3)]
    chunks = width // CHUNK

    def fill(slot_row, pos_row, diag):
        block = pos_t[pl.ds(pos_row, CHUNK), :]
        h_real, h_imag = coupling([block[:, d : d + 1] for d in range(3)], rows, diag)
        for lane, h in ((0, h_real), (width, h_imag)):
            hi, lo = split(h)
            rhs_hi[pl.ds(slot_row, CHUNK), lane : lane + width] = hi
            rhs_lo[pl.ds(slot_row, CHUNK), lane : lane + width] = lo

    lane_ids = lax.broadcasted_iota(jnp.int32, (CHUNK, width), 1)
    sub_ids = lax.broadcasted_iota(jnp.int32, (CHUNK, width), 0)

    def own_chunk(j, carry):
        offset = pl.multiple_of(j * CHUNK, CHUNK)
        fill(offset, pl.multiple_of(my_start + offset, CHUNK), sub_ids + offset == lane_ids)
        return carry

    def other_chunk(j, carry):
        offset = pl.multiple_of(j * CHUNK, CHUNK)
        owner = lax.rem(me + n_row - j // chunks, n_row)
        start = owner * width + lax.rem(j, chunks) * CHUNK
        fill(offset, pl.multiple_of(start, CHUNK), None)
        return carry

    lax.fori_loop(0, chunks, own_chunk, 0)

    col_start = pl.multiple_of(mine * cols, cols)
    own_pos = pos_t[pl.ds(col_start, cols), :]
    own_cols = [own_pos[:, d : d + 1] for d in range(3)]
    slab_diag = lax.broadcasted_iota(jnp.int32, (cols, width), 0) + col_start == lax.broadcasted_iota(
        jnp.int32, (cols, width), 1
    )
    slab_rows = [pos_ref[d : d + 1, :width] for d in range(3)]
    w_real, w_imag = coupling(own_cols, slab_rows, slab_diag)
    w_real = w_real + jnp.where(slab_diag, det_ref[:, :width], 0.0)
    w_imag = w_imag + jnp.where(slab_diag, -0.5, 0.0)
    lead_all = jnp.concatenate([w_real, w_imag], axis=0)

    lax.fori_loop(chunks, n_row * chunks, other_chunk, 0)

    def left(sec, pop):
        signed = jnp.broadcast_to(2.0 * pop - 1.0, (PAD, width))
        return split(jnp.concatenate([sec[0], sec[1], signed], axis=0))

    y_local = sec_ref[...]
    main = jnp.zeros((4 * cols + 2 * PAD, 2 * width), jnp.float32)
    rest = jnp.zeros((2 * cols + PAD, 2 * width), jnp.float32)
    group = 2 if n_row % 2 == 0 else 1
    for first in range(0, n_row, group):
        his, los = [], []
        for s in range(first, first + group):
            if s == 0:
                hi, lo = left(y_local, pop_ref[...])
            else:
                row_copies[s - 1][0].wait_recv()
                row_copies[s - 1][1].wait_recv()
                hi, lo = left(row_buf[s], pop_buf[s])
            his.append(hi)
            los.append(lo)
        hi = jnp.concatenate(his, axis=1)
        lo = jnp.concatenate(los, axis=1)
        span = slice(first * width, (first + group) * width)
        main = main + bdot(jnp.concatenate([hi, lo], axis=0), rhs_hi[span, :])
        rest = rest + bdot(hi, rhs_lo[span, :])
    half = 2 * cols + PAD
    z = main[:half] + main[half:] + rest
    z_real = z[:cols, :width] - z[cols : 2 * cols, width:]
    z_imag = z[:cols, width:] + z[cols : 2 * cols, :width]
    shift = z[2 * cols : 2 * cols + 1, :width]

    for copy in grp_copies:
        copy.wait_recv()
    grp_buf[0] = y_local
    blocks = [grp_buf[lax.rem(mine + n_grp - g, n_grp)] for g in range(n_grp)]
    full = jnp.concatenate(
        [jnp.concatenate([block[0], block[1]], axis=1) for block in blocks], axis=0
    )
    f_hi, f_lo = split(full)
    l_hi, l_lo = split(lead_all[:, :slab])
    v = bdot(l_hi, f_hi) + bdot(l_lo, f_hi) + bdot(l_hi, f_lo)
    v_real = v[:cols, :width] + v[cols:, width:]
    v_imag = v[:cols, width:] - v[cols:, :width]

    y_real, y_imag = y_local[0], y_local[1]
    total_shift = shift + det_ref[:, pl.ds(my_start, width)]
    z_real = z_real + total_shift * y_real + 0.5 * y_imag
    z_imag = z_imag + total_shift * y_imag - 0.5 * y_real
    out_ref[0] = z_imag - v_imag
    out_ref[1] = v_real - z_real

    for copy, pop_copy in row_copies:
        copy.wait_send()
        pop_copy.wait_send()
    for copy in grp_copies:
        copy.wait_send()


def local(positions, detuning, populations, base, section, accum):
    n_row, n_grp = lax.axis_size("row"), lax.axis_size("grp")
    cols, width = section.shape[1], section.shape[2]
    total = positions.shape[1]
    block = section.shape
    rate = pl.pallas_call(
        functools.partial(kernel, n_row, n_grp),
        out_shape=pltpu.VMEM(block, jnp.float32),
        in_specs=[pl.BlockSpec(memory_space=pl.ANY)] * 4,
        out_specs=pl.BlockSpec(memory_space=pltpu.VMEM),
        scratch_shapes=[
            pltpu.VMEM((3, total), jnp.float32),
            pltpu.VMEM((1, total), jnp.float32),
            pltpu.VMEM((1, width), jnp.float32),
            pltpu.VMEM(block, jnp.float32),
            pltpu.VMEM((total, 8), jnp.float32),
            pltpu.VMEM((total, 2 * width), jnp.bfloat16),
            pltpu.VMEM((total, 2 * width), jnp.bfloat16),
            pltpu.VMEM((n_row,) + block, jnp.float32),
            pltpu.VMEM((n_row, 1, width), jnp.float32),
            pltpu.VMEM((n_grp,) + block, jnp.float32),
            pltpu.SemaphoreType.DMA((n_row,)),
            pltpu.SemaphoreType.DMA((n_row,)),
            pltpu.SemaphoreType.DMA((n_row,)),
            pltpu.SemaphoreType.DMA((n_row,)),
            pltpu.SemaphoreType.DMA((n_grp,)),
            pltpu.SemaphoreType.DMA((n_grp,)),
            pltpu.SemaphoreType.DMA((4,)),
        ],
        compiler_params=pltpu.CompilerParams(collective_id=0, has_side_effects=True),
    )(positions, detuning.reshape(1, total), populations.reshape(1, width), section)
    return (base + 0.5 * TIME_STEP * rate, accum + TIME_STEP / 3.0 * rate)


def solution(mesh):
    return jax.shard_map(
        local,
        mesh=mesh,
        in_specs=(
            P(),
            P(),
            P("row"),
            P(None, "grp", "row"),
            P(None, "grp", "row"),
            P(None, "grp", "row"),
        ),
        out_specs=(P(None, "grp", "row"), P(None, "grp", "row")),
        check_vma=False,
    )
```

profile of v0, /device:TPU:0, one launch (start us, length us, event | category | flops | bytes accessed | tf_op | source)
XLA Modules:
  0.0 12.3 jit_solution(16905267959714192407)
XLA Ops:
  0.6 0.0 copy-start
  0.6 0.0 copy-start.1
  0.7 11.0 %shard_map.77 = f32[2,16,128]{2,1,0:T(8,128)S(1)} custom-call(f32[3,1024]{1,0:T(4,128)} %pos_in.1, f32[1,1024]{1,0:T(1,128)} %bitcast.2, f32[1,128]{1,0:T(1,128)} %bitcast.3, f32[2,16,128]{2,1,0:T(8,128)} %sec_in.1), custom_call_target="tpu_custom_call" | custom-call | tf_op jit(solution)/shard_map/pallas_call | solution.py:270
  11.7 0.0 copy-done
  11.7 0.0 copy-done.1
  11.7 0.6 %multiply_add_fusion = (f32[2,16,128]{2,1,0:T(8,128)}, f32[2,16,128]{2,1,0:T(8,128)}) fusion(f32[2,16,128]{2,1,0:T(8,128)S(1)} %copy-done, f32[2,16,128]{2,1,0:T(8,128)S(1)} %shard_map.77, f32[2,16,128]{2,1,0:T(8,128)S(1)} %copy-done.1), kind=kLoop, calls=%fused_computation | loop fusion | flops 16384 | bytes 81920 | tf_op jit(solution)/shard_map/add | solution.py:296
Async XLA Ops:
  0.6 11.0 %copy-start = (f32[2,16,128]{2,1,0:T(8,128)S(1)}, f32[2,16,128]{2,1,0:T(8,128)}, u32[]{:S(2)}) copy-start(f32[2,16,128]{2,1,0:T(8,128)} %param.11) | copy-start | bytes 49156
  0.6 11.0 %copy-start.1 = (f32[2,16,128]{2,1,0:T(8,128)S(1)}, f32[2,16,128]{2,1,0:T(8,128)}, u32[]{:S(2)}) copy-start(f32[2,16,128]{2,1,0:T(8,128)} %param.9) | copy-start | bytes 49156
where the time goes:
time: 12.5 us; the launch traced here: 12.3 us
  Pallas kernels  11 us (88%)
  between operations  0.67 us (5%)
  other arithmetic  0.62 us (5%)
    pallas_call x1, Pallas kernels, local(): pl.pallas_call(functools.partial(kernel, n_row, n_grp), out_shape=pltpu.V...  11 us
    add x1, other arithmetic, local(): return (base + 0.5 * TIME_STEP * rate, accum + TIME_STEP / 3.0 * rate)  0.62 us

commit v1 on v0

--- a/solution.py
+++ b/solution.py
@@ -88,30 +88,34 @@
     out_ref,
     pos_ref,
     det_ref,
-    pop_ref,
-    sec_ref,
+    stage,
     pos_t,
     rhs_hi,
     rhs_lo,
     row_buf,
-    pop_buf,
     grp_buf,
     sec_send,
     sec_recv,
-    pop_send,
-    pop_recv,
     grp_send,
     grp_recv,
     load_sem,
 ):
+    cols, width = sec_in.shape[1], sec_in.shape[2]
     loads = []
-    for i, (src, dst) in enumerate(((sec_in, sec_ref), (pop_in, pop_ref), (pos_in, pos_ref), (det_in, det_ref))):
+    for i, (src, dst) in enumerate(
+        (
+            (sec_in.at[0], stage.at[0:cols]),
+            (sec_in.at[1], stage.at[cols : 2 * cols]),
+            (pop_in, stage.at[2 * cols : 2 * cols + 1]),
+            (pos_in, pos_ref),
+            (det_in, det_ref),
+        )
+    ):
         load = pltpu.make_async_copy(src, dst, load_sem.at[i])
         load.start()
         loads.append(load)
     me = lax.axis_index("row")
     mine = lax.axis_index("grp")
-    cols, width = sec_ref.shape[1], sec_ref.shape[2]
     slab = cols * n_grp
 
     def row_peer(s):
@@ -121,31 +125,20 @@
         return lax.rem(mine + s, n_grp)
 
     barrier = pltpu.get_barrier_semaphore()
+    for s in range(1, n_grp):
+        pl.semaphore_signal(barrier, inc=1, device_id={"grp": grp_peer(s)}, device_id_type=pl.DeviceIdType.MESH)
     for s in range(1, n_row):
         pl.semaphore_signal(barrier, inc=1, device_id={"row": row_peer(s)}, device_id_type=pl.DeviceIdType.MESH)
-    for s in range(1, n_grp):
-        pl.semaphore_signal(barrier, inc=1, device_id={"grp": grp_peer(s)}, device_id_type=pl.DeviceIdType.MESH)
 
     loads[0].wait()
     loads[1].wait()
     pl.semaphore_wait(barrier, n_row + n_grp - 2)
 
-    row_copies = []
-    for s in range(1, n_row):
-        target = {"row": row_peer(s)}
-        copy = pltpu.make_async_remote_copy(
-            sec_ref, row_buf.at[s], sec_send.at[s], sec_recv.at[s], device_id=target, device_id_type=pl.DeviceIdType.MESH
-        )
-        copy.start()
-        pop_copy = pltpu.make_async_remote_copy(
-            pop_ref, pop_buf.at[s], pop_send.at[s], pop_recv.at[s], device_id=target, device_id_type=pl.DeviceIdType.MESH
-        )
-        pop_copy.start()
-        row_copies.append((copy, pop_copy))
+    slab_part = stage.at[0 : 2 * cols]
     grp_copies = []
     for s in range(1, n_grp):
         copy = pltpu.make_async_remote_copy(
-            sec_ref,
+            slab_part,
             grp_buf.at[s],
             grp_send.at[s],
             grp_recv.at[s],
@@ -154,9 +147,22 @@
         )
         copy.start()
         grp_copies.append(copy)
-
     loads[2].wait()
+    row_copies = []
+    for s in range(n_row - 1, 0, -1):
+        copy = pltpu.make_async_remote_copy(
+            stage,
+            row_buf.at[s],
+            sec_send.at[s],
+            sec_recv.at[s],
+            device_id={"row": row_peer(s)},
+            device_id_type=pl.DeviceIdType.MESH,
+        )
+        copy.start()
+        row_copies.insert(0, copy)
+
     loads[3].wait()
+    loads[4].wait()
     for b in range(n_row):
         part = pos_ref[:, b * width : (b + 1) * width]
         tall = jnp.concatenate([part, jnp.zeros((5, width), jnp.float32)], axis=0)
@@ -203,13 +209,13 @@
     w_imag = w_imag + jnp.where(slab_diag, -0.5, 0.0)
     lead_all = jnp.concatenate([w_real, w_imag], axis=0)
 
-    lax.fori_loop(chunks, n_row * chunks, other_chunk, 0)
-
-    def left(sec, pop):
-        signed = jnp.broadcast_to(2.0 * pop - 1.0, (PAD, width))
-        return split(jnp.concatenate([sec[0], sec[1], signed], axis=0))
-
-    y_local = sec_ref[...]
+    lax.fori_loop(chunks, n_row * chunks, other_chunk, 0, unroll=2)
+
+    def left(slab_and_pop):
+        signed = jnp.broadcast_to(2.0 * slab_and_pop[2 * cols :] - 1.0, (PAD, width))
+        return split(jnp.concatenate([slab_and_pop[: 2 * cols], signed], axis=0))
+
+    y_local = stage[0 : 2 * cols]
     main = jnp.zeros((4 * cols + 2 * PAD, 2 * width), jnp.float32)
     rest = jnp.zeros((2 * cols + PAD, 2 * width), jnp.float32)
     group = 2 if n_row % 2 == 0 else 1
@@ -217,11 +223,10 @@
         his, los = [], []
         for s in range(first, first + group):
             if s == 0:
-                hi, lo = left(y_local, pop_ref[...])
+                hi, lo = left(stage[...])
             else:
-                row_copies[s - 1][0].wait_recv()
-                row_copies[s - 1][1].wait_recv()
-                hi, lo = left(row_buf[s], pop_buf[s])
+                row_copies[s - 1].wait_recv()
+                hi, lo = left(row_buf[s])
             his.append(hi)
             los.append(lo)
         hi = jnp.concatenate(his, axis=1)
@@ -240,7 +245,7 @@
     grp_buf[0] = y_local
     blocks = [grp_buf[lax.rem(mine + n_grp - g, n_grp)] for g in range(n_grp)]
     full = jnp.concatenate(
-        [jnp.concatenate([block[0], block[1]], axis=1) for block in blocks], axis=0
+        [jnp.concatenate([block[:cols], block[cols:]], axis=1) for block in blocks], axis=0
     )
     f_hi, f_lo = split(full)
     l_hi, l_lo = split(lead_all[:, :slab])
@@ -248,17 +253,14 @@
     v_real = v[:cols, :width] + v[cols:, width:]
     v_imag = v[:cols, width:] - v[cols:, :width]
 
-    y_real, y_imag = y_local[0], y_local[1]
+    y_real, y_imag = y_local[:cols], y_local[cols:]
     total_shift = shift + det_ref[:, pl.ds(my_start, width)]
     z_real = z_real + total_shift * y_real + 0.5 * y_imag
     z_imag = z_imag + total_shift * y_imag - 0.5 * y_real
     out_ref[0] = z_imag - v_imag
     out_ref[1] = v_real - z_real
 
-    for copy, pop_copy in row_copies:
-        copy.wait_send()
-        pop_copy.wait_send()
-    for copy in grp_copies:
+    for copy in row_copies + grp_copies:
         copy.wait_send()
 
 
@@ -275,21 +277,17 @@
         scratch_shapes=[
             pltpu.VMEM((3, total), jnp.float32),
             pltpu.VMEM((1, total), jnp.float32),
-            pltpu.VMEM((1, width), jnp.float32),
-            pltpu.VMEM(block, jnp.float32),
+            pltpu.VMEM((2 * cols + 1, width), jnp.float32),
             pltpu.VMEM((total, 8), jnp.float32),
             pltpu.VMEM((total, 2 * width), jnp.bfloat16),
             pltpu.VMEM((total, 2 * width), jnp.bfloat16),
-            pltpu.VMEM((n_row,) + block, jnp.float32),
-            pltpu.VMEM((n_row, 1, width), jnp.float32),
-            pltpu.VMEM((n_grp,) + block, jnp.float32),
-            pltpu.SemaphoreType.DMA((n_row,)),
-            pltpu.SemaphoreType.DMA((n_row,)),
+            pltpu.VMEM((n_row, 2 * cols + 1, width), jnp.float32),
+            pltpu.VMEM((n_grp, 2 * cols, width), jnp.float32),
             pltpu.SemaphoreType.DMA((n_row,)),
             pltpu.SemaphoreType.DMA((n_row,)),
             pltpu.SemaphoreType.DMA((n_grp,)),
             pltpu.SemaphoreType.DMA((n_grp,)),
-            pltpu.SemaphoreType.DMA((4,)),
+            pltpu.SemaphoreType.DMA((5,)),
         ],
         compiler_params=pltpu.CompilerParams(collective_id=0, has_side_effects=True),
     )(positions, detuning.reshape(1, total), populations.reshape(1, width), section)

time: 12.5 us -> 12.4 us (level)
  no operation moved by 1% of the time
where the time goes in v1:
time: 12.4 us; the launch traced here: 12.2 us
  Pallas kernels  10.9 us (88%)
  between operations  0.67 us (5%)
  other arithmetic  0.62 us (5%)
    pallas_call x1, Pallas kernels, local(): pl.pallas_call(functools.partial(kernel, n_row, n_grp), out_shape=pltpu.V...  10.9 us
    add x1, other arithmetic, local(): return (base + 0.5 * TIME_STEP * rate, accum + TIME_STEP / 3.0 * rate)  0.62 us

profile of v1, /device:TPU:0, one launch (start us, length us, event | category | flops | bytes accessed | tf_op | source)
XLA Modules:
  0.0 12.2 jit_solution(10310155631430797678)
XLA Ops:
  0.6 0.0 copy-start
  0.6 0.0 copy-start.1
  0.7 10.9 %shard_map.77 = f32[2,16,128]{2,1,0:T(8,128)S(1)} custom-call(f32[3,1024]{1,0:T(4,128)} %pos_in.1, f32[1,1024]{1,0:T(1,128)} %bitcast.2, f32[1,128]{1,0:T(1,128)} %bitcast.3, f32[2,16,128]{2,1,0:T(8,128)} %sec_in.1), custom_call_target="tpu_custom_call" | custom-call | tf_op jit(solution)/shard_map/pallas_call | solution.py:272
  11.6 0.0 copy-done
  11.6 0.0 copy-done.1
  11.6 0.6 %multiply_add_fusion = (f32[2,16,128]{2,1,0:T(8,128)}, f32[2,16,128]{2,1,0:T(8,128)}) fusion(f32[2,16,128]{2,1,0:T(8,128)S(1)} %copy-done, f32[2,16,128]{2,1,0:T(8,128)S(1)} %shard_map.77, f32[2,16,128]{2,1,0:T(8,128)S(1)} %copy-done.1), kind=kLoop, calls=%fused_computation | loop fusion | flops 16384 | bytes 81920 | tf_op jit(solution)/shard_map/add | solution.py:294
Async XLA Ops:
  0.6 11.0 %copy-start = (f32[2,16,128]{2,1,0:T(8,128)S(1)}, f32[2,16,128]{2,1,0:T(8,128)}, u32[]{:S(2)}) copy-start(f32[2,16,128]{2,1,0:T(8,128)} %param.11) | copy-start | bytes 49156
  0.6 11.0 %copy-start.1 = (f32[2,16,128]{2,1,0:T(8,128)S(1)}, f32[2,16,128]{2,1,0:T(8,128)}, u32[]{:S(2)}) copy-start(f32[2,16,128]{2,1,0:T(8,128)} %param.9) | copy-start | bytes 49156

commit v2 on v1

--- a/solution.py
+++ b/solution.py
@@ -125,15 +125,28 @@
         return lax.rem(mine + s, n_grp)
 
     barrier = pltpu.get_barrier_semaphore()
+    for s in range(1, n_row):
+        pl.semaphore_signal(barrier, inc=1, device_id={"row": row_peer(s)}, device_id_type=pl.DeviceIdType.MESH)
     for s in range(1, n_grp):
         pl.semaphore_signal(barrier, inc=1, device_id={"grp": grp_peer(s)}, device_id_type=pl.DeviceIdType.MESH)
-    for s in range(1, n_row):
-        pl.semaphore_signal(barrier, inc=1, device_id={"row": row_peer(s)}, device_id_type=pl.DeviceIdType.MESH)
 
     loads[0].wait()
     loads[1].wait()
     pl.semaphore_wait(barrier, n_row + n_grp - 2)
 
+    loads[2].wait()
+    row_copies = {}
+    for s in range(1, n_row):
+        copy = pltpu.make_async_remote_copy(
+            stage,
+            row_buf.at[s],
+            sec_send.at[s],
+            sec_recv.at[s],
+            device_id={"row": row_peer(s)},
+            device_id_type=pl.DeviceIdType.MESH,
+        )
+        copy.start()
+        row_copies[s] = copy
     slab_part = stage.at[0 : 2 * cols]
     grp_copies = []
     for s in range(1, n_grp):
@@ -147,19 +160,6 @@
         )
         copy.start()
         grp_copies.append(copy)
-    loads[2].wait()
-    row_copies = []
-    for s in range(n_row - 1, 0, -1):
-        copy = pltpu.make_async_remote_copy(
-            stage,
-            row_buf.at[s],
-            sec_send.at[s],
-            sec_recv.at[s],
-            device_id={"row": row_peer(s)},
-            device_id_type=pl.DeviceIdType.MESH,
-        )
-        copy.start()
-        row_copies.insert(0, copy)
 
     loads[3].wait()
     loads[4].wait()
@@ -225,7 +225,7 @@
             if s == 0:
                 hi, lo = left(stage[...])
             else:
-                row_copies[s - 1].wait_recv()
+                row_copies[s].wait_recv()
                 hi, lo = left(row_buf[s])
             his.append(hi)
             los.append(lo)
@@ -260,7 +260,7 @@
     out_ref[0] = z_imag - v_imag
     out_ref[1] = v_real - z_real
 
-    for copy in row_copies + grp_copies:
+    for copy in list(row_copies.values()) + grp_copies:
         copy.wait_send()
 
 

time: 12.4 us -> 11.9 us (0.960)
  Pallas kernels: 10.9 us -> 10.5 us
    pallas_call x1, Pallas kernels: 10.9 us -> 10.5 us  [local(): pl.pallas_call(functools.partial(kernel, n_row, n_grp), out_shape=pltpu.V...]
where the time goes in v2:
time: 11.9 us; the launch traced here: 11.8 us
  Pallas kernels  10.5 us (88%)
  between operations  0.67 us (6%)
  other arithmetic  0.62 us (5%)
    pallas_call x1, Pallas kernels, local(): pl.pallas_call(functools.partial(kernel, n_row, n_grp), out_shape=pltpu.V...  10.5 us
    add x1, other arithmetic, local(): return (base + 0.5 * TIME_STEP * rate, accum + TIME_STEP / 3.0 * rate)  0.62 us

profile of v2, /device:TPU:0, one launch (start us, length us, event | category | flops | bytes accessed | tf_op | source)
XLA Modules:
  0.0 11.8 jit_solution(3427077061657421365)
XLA Ops:
  0.6 0.0 copy-start
  0.6 0.0 copy-start.1
  0.7 10.5 %shard_map.77 = f32[2,16,128]{2,1,0:T(8,128)S(1)} custom-call(f32[3,1024]{1,0:T(4,128)} %pos_in.1, f32[1,1024]{1,0:T(1,128)} %bitcast.2, f32[1,128]{1,0:T(1,128)} %bitcast.3, f32[2,16,128]{2,1,0:T(8,128)} %sec_in.1), custom_call_target="tpu_custom_call" | custom-call | tf_op jit(solution)/shard_map/pallas_call | solution.py:272
  11.1 0.0 copy-done
  11.1 0.0 copy-done.1
  11.1 0.6 %multiply_add_fusion = (f32[2,16,128]{2,1,0:T(8,128)}, f32[2,16,128]{2,1,0:T(8,128)}) fusion(f32[2,16,128]{2,1,0:T(8,128)S(1)} %copy-done, f32[2,16,128]{2,1,0:T(8,128)S(1)} %shard_map.77, f32[2,16,128]{2,1,0:T(8,128)S(1)} %copy-done.1), kind=kLoop, calls=%fused_computation | loop fusion | flops 16384 | bytes 81920 | tf_op jit(solution)/shard_map/add | solution.py:294
Async XLA Ops:
  0.6 10.5 %copy-start = (f32[2,16,128]{2,1,0:T(8,128)S(1)}, f32[2,16,128]{2,1,0:T(8,128)}, u32[]{:S(2)}) copy-start(f32[2,16,128]{2,1,0:T(8,128)} %param.11) | copy-start | bytes 49156
  0.6 10.5 %copy-start.1 = (f32[2,16,128]{2,1,0:T(8,128)S(1)}, f32[2,16,128]{2,1,0:T(8,128)}, u32[]{:S(2)}) copy-start(f32[2,16,128]{2,1,0:T(8,128)} %param.9) | copy-start | bytes 49156
